TPU v7x, 32 devices: a whole 2x2x4 slice. The times are simulated.
32 devices in a mesh: dp: 8 (over y, x, core), own: 4 (over z).
Axes of the slice: x: 2, y: 2, z: 4, core: 2. Of those that a mesh axis runs over, the one named last changes fastest.
Arguments:
- grad: bfloat16 [8192, 1024], P(('dp', 'own')), may hold values from -88 to 88
- left_stats: float32 [8, 1024, 1024], P('dp', 'own'), may hold values from -0.4 to 2.6
- right_stats: float32 [8, 1024, 1024], P('dp', 'own'), may hold values from -0.4 to 2.6
- left_roots: float32 [8, 1024, 1024], P('dp', 'own'), may hold values from -0.4 to 2.6, as said below
- right_roots: float32 [8, 1024, 1024], P('dp', 'own'), may hold values from -0.4 to 2.6, as said below
Outputs:
- direction: bfloat16 [8192, 1024], P(('dp', 'own'))
- left_new: float32 [8, 1024, 1024], P('dp', 'own')
- right_new: float32 [8, 1024, 1024], P('dp', 'own')
Inputs may be any that keep to these rules, and one draw needn't show every extreme that they name: `right_roots`: each block's feature-side root is symmetric. `left_roots`: each block's vocabulary-side root is symmetric.
All inputs are finite; a program needn't handle non-finite values.
Results may differ from a plain program's by a relative error of at most 0.0049.
Values may be sent and summed in bfloat16 or wider, within the bound.
No kernel may reach another device: no remote copies, remote signals or barrier semaphores. Data moves between devices by JAX's collectives and lax.ppermute only.
A program may use at most 64 MiB of HBM per device.

v0:
```python
import jax
import jax.numpy as jnp
from jax import lax
from jax.sharding import PartitionSpec as P

highest = lax.Precision.HIGHEST
epsilon = 1e-06


def transpose_product(left_side, right_side):
    return lax.dot_general(
        left_side, right_side, (((0,), (0,)), ((), ())), preferred_element_type=jnp.float32
    )


def local(grad, left_stats, right_stats, left_roots, right_roots):
    feature_width = grad.shape[1]
    owner_count = lax.axis_size("own")
    slice_width = feature_width // owner_count
    own_rows = grad.astype(jnp.float32)
    grad_square = jnp.sum(own_rows * own_rows)
    whole_grad = lax.all_gather(grad, "own", axis=0, tiled=True)
    feature_cols = lax.dynamic_slice_in_dim(
        whole_grad, lax.axis_index("own") * slice_width, slice_width, 1
    )
    left_gram = lax.dot_general(
        grad, whole_grad, (((1,), (1,)), ((), ())), preferred_element_type=jnp.float32
    )
    right_gram = transpose_product(feature_cols, whole_grad)
    left_update = 0.9 * left_stats[0] + 0.1 / feature_width * left_gram
    right_update = 0.9 * right_stats[0] + 0.1 / feature_width * right_gram
    mixed_cols = lax.dot_general(
        whole_grad.astype(jnp.float32), right_roots[0], (((1,), (1,)), ((), ())), precision=highest
    )
    mixed_cols = mixed_cols.astype(jnp.bfloat16)
    precond = jnp.dot(
        left_roots[0],
        lax.all_gather(mixed_cols, "own", axis=1, tiled=True).astype(jnp.float32),
        precision=highest,
    )
    precond_square = jnp.sum(precond * precond)
    norm_totals = lax.psum((grad_square, precond_square), "own")
    graft_scale = jnp.sqrt(norm_totals[0] / (norm_totals[1] + epsilon))
    direction = (precond * graft_scale).astype(jnp.bfloat16)
    return (direction, left_update[None], right_update[None])


def solution(mesh):
    in_specs = (
        P(("dp", "own"), None),
        P("dp", "own", None),
        P("dp", "own", None),
        P("dp", "own", None),
        P("dp", "own", None),
    )
    out_specs = (P(("dp", "own"), None), P("dp", "own", None), P("dp", "own", None))
    return jax.shard_map(local, mesh=mesh, in_specs=in_specs, out_specs=out_specs, check_vma=False)
```

profile of v0, /device:TPU:0, one launch (start us, length us, event | category | flops | bytes accessed | tf_op | source)
XLA Modules:
  0.0 131.7 jit_solution(18139367668326251888)
XLA Ops:
  7.2 0.0 copy-start
  7.2 0.0 all-gather.3.cloned.1.call-start
  7.2 0.7 all-gather.3.cloned.1.call-update
  7.9 0.0 all-gather.5.cloned.1.call-start
  8.0 50.0 %all-gather.3.cloned.1.call-done = bf16[1024,1024]{1,0:T(8,128)(2,1)} async-done(((bf16[256,1024]{1,0:T(8,128)(2,1)}), bf16[1024,1024]{1,0:T(8,128)(2,1)}) %all-gather.3.cloned.1.call-update) | async-done | bytes 2097168 | tf_op jit(solution)/shard_map/all_gather | solution.py:22
  58.0 0.0 copy-start.1
  58.0 4.7 %convolution_convert_fusion = bf16[1024,256]{1,0:T(8,128)(2,1)} fusion(bf16[1024,1024]{1,0:T(8,128)(2,1)} %all-gather.3.cloned.1.call-done, f32[1,256,1024]{2,1,0:T(8,128)} %param.9), kind=kOutput, calls=%fused_computation.6 | convolution fusion | flops 3221487616 | bytes 3670016 | tf_op jit(solution)/shard_map/dot_general | solution.py:32
  62.6 0.0 all-gather.5.cloned.1.call-update
  62.7 1.9 %multiply_reduce_fusion.1 = f32[]{:T(128)} fusion(bf16[256,1024]{1,0:T(8,128)(2,1)} %param.5), kind=kLoop, calls=%fused_computation.12 | loop fusion | flops 786431 | bytes 524292 | tf_op jit(solution)/shard_map/reduce_sum | solution.py:21
  64.6 0.0 copy-done.1
  64.6 0.0 copy-start.2
  64.6 0.0 copy-start.3
  64.6 3.1 %fusion.1 = f32[1,256,1024]{2,1,0:T(8,128)} fusion(bf16[1024,1024]{1,0:T(8,128)(2,1)S(1)} %copy-done.1, f32[1,256,1024]{2,1,0:T(8,128)} %param.7, s32[]{:T(128)S(6)} %select_n.3), kind=kOutput, calls=%fused_computation.2 | convolution fusion | flops 537657344 | bytes 4718596 | tf_op jit(solution)/shard_map/dot_general | solution.py:11
  67.7 0.0 copy-done.2
  67.7 0.0 copy-done.3
  67.7 1.8 %fusion.3 = f32[1,256,1024]{2,1,0:T(8,128)} fusion(bf16[256,1024]{1,0:T(8,128)(2,1)S(1)} %copy-done.2, bf16[1024,1024]{1,0:T(8,128)(2,1)S(1)} %copy-done.1, f32[1,256,1024]{2,1,0:T(8,128)S(1)} %copy-done.3), kind=kOutput, calls=%fused_computation.5 | convolution fusion | flops 537657344 | bytes 4718592 | tf_op jit(solution)/shard_map/dot_general | solution.py:26
  69.4 38.4 %all-gather.5.cloned.1.call-done = bf16[1024,1024]{1,0:T(8,128)(2,1)} async-done(((bf16[1024,256]{1,0:T(8,128)(2,1)}), bf16[1024,1024]{1,0:T(8,128)(2,1)}) %all-gather.5.cloned.1.call-update) | async-done | bytes 2097168 | tf_op jit(solution)/shard_map/all_gather | solution.py:38
  107.9 0.0 copy-done
  107.9 4.6 %multiply_reduce_fusion = (f32[]{:T(128)}, f32[1024,256]{1,0:T(8,128)S(1)}) fusion(bf16[1024,1024]{1,0:T(8,128)(2,1)} %all-gather.5.cloned.1.call-done, f32[1,256,1024]{2,1,0:T(8,128)S(1)} %copy-done), kind=kOutput, calls=%fused_computation.11 | convolution fusion | flops 3221749760 | bytes 4194308 | tf_op jit(solution)/shard_map/dot_general | solution.py:36
  112.4 10.0 %all-reduce = (f32[]{:T(128)}, f32[]{:T(128)}) all-reduce(f32[]{:T(128)} %multiply_reduce_fusion.1, f32[]{:T(128)} %get-tuple-element.8), channel_id=1, replica_groups=mesh['dp'=8,'own'=4] {'own'}, use_global_device_ids=true, to_apply=%region_1.0 | all-reduce | flops 2 | bytes 16 | tf_op jit(solution)/shard_map/psum | solution.py:42
  123.7 0.1 fusion.7
  123.9 1.0 copy.8
Async XLA Ops:
  7.2 100.7 %copy-start = (f32[1,256,1024]{2,1,0:T(8,128)S(1)}, f32[1,256,1024]{2,1,0:T(8,128)}, u32[]{:S(2)}) copy-start(f32[1,256,1024]{2,1,0:T(8,128)} %param.8) | copy-start | bytes 3145732
  7.2 50.8 %all-gather.3.cloned.1.call-start = ((), (), s32[]{:S(2)}) async-start(), calls=%async_computation | async-start | bytes 2621440 | tf_op jit(solution)/shard_map/all_gather | solution.py:22
  7.9 100.0 %all-gather.5.cloned.1.call-start = ((), (), s32[]{:S(2)}) async-start(), calls=%async_computation.1 | async-start | bytes 2621440 | tf_op jit(solution)/shard_map/all_gather | solution.py:38
  58.0 6.6 %copy-start.1 = (bf16[1024,1024]{1,0:T(8,128)(2,1)S(1)}, bf16[1024,1024]{1,0:T(8,128)(2,1)}, u32[]{:S(2)}) copy-start(bf16[1024,1024]{1,0:T(8,128)(2,1)} %all-gather.3.cloned.1.call-done) | copy-start | bytes 6291460
  64.6 3.1 %copy-start.2 = (bf16[256,1024]{1,0:T(8,128)(2,1)S(1)}, bf16[256,1024]{1,0:T(8,128)(2,1)}, u32[]{:S(2)}) copy-start(bf16[256,1024]{1,0:T(8,128)(2,1)} %param.5) | copy-start | bytes 1572868
  64.6 3.1 %copy-start.3 = (f32[1,256,1024]{2,1,0:T(8,128)S(1)}, f32[1,256,1024]{2,1,0:T(8,128)}, u32[]{:S(2)}) copy-start(f32[1,256,1024]{2,1,0:T(8,128)} %param.6) | copy-start | bytes 3145732
Sparse Core Ops, SparseCore 0:
  9.6 48.3 all-gather.2
  62.8 45.0 all-gather.4
where the time goes:
time: 132 us
  waiting for transfers between devices  89.2 us (68%)
  between operations  15.3 us (12%)
  matrix products  14.1 us (11%)
  blocking collectives  10 us (8%)
  other arithmetic  2.01 us (2%)
    all_gather x1, waiting for transfers between devices, local(): whole_grad = lax.all_gather(grad, 'own', axis=0, tiled=True)  50 us
    all_gather x1, waiting for transfers between devices, local(): lax.all_gather(mixed_cols, 'own', axis=1, tiled=True).astype(jnp.float32)  38.4 us
    psum x1, blocking collectives, local(): norm_totals = lax.psum((grad_square, precond_square), 'own')  10 us
    dot_general x1, matrix products, local(): lax.dot_general(whole_grad.astype(jnp.float32), right_roots[0], (((1,), (...  4.66 us
    dot_general x1, matrix products, local(): jnp.dot(left_roots[0], lax.all_gather(mixed_cols, 'own', axis=1, tiled=Tr...  4.57 us
    dot_general x1, matrix products, transpose_product(): lax.dot_general(left_side, right_side, (((0,), (0,)), ((), ())), preferre...  3.07 us
  transfers between devices with their start and end apart: 2, of which 2 were waited for; matrix products, arithmetic and copies ran while one was open for 5% of the time, Pallas kernels for 0%

commit v1 on v0

--- a/solution.py
+++ b/solution.py
@@ -35,7 +35,7 @@
     mixed_cols = mixed_cols.astype(jnp.bfloat16)
     precond = jnp.dot(
         left_roots[0],
-        lax.all_gather(mixed_cols, "own", axis=1, tiled=True).astype(jnp.float32),
+        jnp.concatenate(lax.all_gather(mixed_cols, "own"), axis=1).astype(jnp.float32),
         precision=highest,
     )
     precond_square = jnp.sum(precond * precond)

time: 132 us -> 135 us (1.023)
  local copies, waits for them, and re-layouts: 1.02 us -> 4.01 us
    all_gather x0 -> x1, local copies, waits for them, and re-layouts: none -> 2.99 us  [local(): lax.all_gather(mixed_cols, 'own')]
where the time goes in v1:
time: 135 us; the launch traced here: 134 us
  waiting for transfers between devices  88.6 us (66%)
  between operations  15.3 us (11%)
  matrix products  12.9 us (10%)
  blocking collectives  10.3 us (8%)
  local copies, waits for them, and re-layouts  4.01 us (3%)
  other arithmetic  3.22 us (2%)
    all_gather x1, waiting for transfers between devices, local(): whole_grad = lax.all_gather(grad, 'own', axis=0, tiled=True)  50 us
    all_gather x1, waiting for transfers between devices, local(): lax.all_gather(mixed_cols, 'own')  37.8 us
    psum x1, blocking collectives, local(): norm_totals = lax.psum((grad_square, precond_square), 'own')  10.3 us
    dot_general x1, matrix products, local(): lax.dot_general(whole_grad.astype(jnp.float32), right_roots[0], (((1,), (...  4.66 us
    dot_general x1, matrix products, local(): jnp.dot(left_roots[0], jnp.concatenate(lax.all_gather(mixed_cols, 'own'),...  3.43 us
    dot_general x1, matrix products, transpose_product(): lax.dot_general(left_side, right_side, (((0,), (0,)), ((), ())), preferre...  3.07 us
    all_gather x1, local copies, waits for them, and re-layouts, local(): lax.all_gather(mixed_cols, 'own')  2.99 us
  transfers between devices with their start and end apart: 2, of which 2 were waited for; matrix products, arithmetic and copies ran while one was open for 5% of the time, Pallas kernels for 0%

profile of v1, /device:TPU:0, one launch (start us, length us, event | category | flops | bytes accessed | tf_op | source)
XLA Modules:
  0.0 134.5 jit_solution(7012965665412155063)
XLA Ops:
  7.2 0.0 copy-start
  7.2 0.0 all-gather.4.cloned.1.call-start
  7.2 0.7 all-gather.4.cloned.1.call-update
  7.9 0.0 all-gather.6.cloned.1.call-start
  8.0 50.0 %all-gather.4.cloned.1.call-done = bf16[1024,1024]{1,0:T(8,128)(2,1)} async-done(((bf16[256,1024]{1,0:T(8,128)(2,1)}), bf16[1024,1024]{1,0:T(8,128)(2,1)}) %all-gather.4.cloned.1.call-update) | async-done | bytes 2097168 | tf_op jit(solution)/shard_map/all_gather | solution.py:22
  58.0 0.0 copy-start.1
  58.0 4.7 %convolution_convert_fusion = bf16[1024,256]{1,0:T(8,128)(2,1)} fusion(bf16[1024,1024]{1,0:T(8,128)(2,1)} %all-gather.4.cloned.1.call-done, f32[1,256,1024]{2,1,0:T(8,128)} %param.9), kind=kOutput, calls=%fused_computation.6 | convolution fusion | flops 3221487616 | bytes 3670016 | tf_op jit(solution)/shard_map/dot_general | solution.py:32
  62.6 0.0 all-gather.6.cloned.1.call-update
  62.7 1.9 %multiply_reduce_fusion.1 = f32[]{:T(128)} fusion(bf16[256,1024]{1,0:T(8,128)(2,1)} %param.5), kind=kLoop, calls=%fused_computation.12 | loop fusion | flops 786431 | bytes 524292 | tf_op jit(solution)/shard_map/reduce_sum | solution.py:21
  64.6 0.0 copy-done.1
  64.6 0.0 copy-start.2
  64.6 0.0 copy-start.3
  64.6 3.1 %fusion.1 = f32[1,256,1024]{2,1,0:T(8,128)} fusion(bf16[1024,1024]{1,0:T(8,128)(2,1)S(1)} %copy-done.1, f32[1,256,1024]{2,1,0:T(8,128)} %param.7, s32[]{:T(128)S(6)} %select_n.3), kind=kOutput, calls=%fused_computation.2 | convolution fusion | flops 537657344 | bytes 4718596 | tf_op jit(solution)/shard_map/dot_general | solution.py:11
  67.7 0.0 copy-done.2
  67.7 0.0 copy-done.3
  67.7 1.8 %fusion.3 = f32[1,256,1024]{2,1,0:T(8,128)} fusion(bf16[256,1024]{1,0:T(8,128)(2,1)S(1)} %copy-done.2, bf16[1024,1024]{1,0:T(8,128)(2,1)S(1)} %copy-done.1, f32[1,256,1024]{2,1,0:T(8,128)S(1)} %copy-done.3), kind=kOutput, calls=%fused_computation.5 | convolution fusion | flops 537657344 | bytes 4718592 | tf_op jit(solution)/shard_map/dot_general | solution.py:26
  69.4 37.8 %all-gather.6.cloned.1.call-done = bf16[4096,256]{1,0:T(8,128)(2,1)} async-done(((bf16[1024,256]{1,0:T(8,128)(2,1)}), bf16[4096,256]{1,0:T(8,128)(2,1)}) %all-gather.6.cloned.1.call-update) | async-done | bytes 2097168 | tf_op jit(solution)/shard_map/all_gather | solution.py:38
  107.3 3.0 %copy.9 = bf16[4,1024,256]{1,2,0:T(8,128)(2,1)S(1)} copy(bf16[4,1024,256]{2,1,0:T(8,128)(2,1)} %bitcast.28) | data formatting | bytes 4194304 | tf_op jit(solution)/shard_map/all_gather | solution.py:38
  110.3 0.0 copy-done
  110.3 3.4 %multiply_reduce_fusion = (f32[]{:T(128)}, f32[1024,256]{1,0:T(8,128)}) fusion(bf16[1024,1024]{0,1:T(8,128)(2,1)S(1)} %bitcast.27, f32[1,256,1024]{2,1,0:T(8,128)S(1)} %copy-done), kind=kOutput, calls=%fused_computation.11 | convolution fusion | flops 3221749760 | bytes 4194308 | tf_op jit(solution)/shard_map/dot_general | solution.py:36
  113.7 10.3 %all-reduce = (f32[]{:T(128)}, f32[]{:T(128)}) all-reduce(f32[]{:T(128)} %multiply_reduce_fusion.1, f32[]{:T(128)} %get-tuple-element.11), channel_id=1, replica_groups=mesh['dp'=8,'own'=4] {'own'}, use_global_device_ids=true, to_apply=%region_1.0 | all-reduce | flops 2 | bytes 16 | tf_op jit(solution)/shard_map/psum | solution.py:42
  125.3 1.3 fusion.7
  126.6 1.0 copy.10
Async XLA Ops:
  7.2 103.1 %copy-start = (f32[1,256,1024]{2,1,0:T(8,128)S(1)}, f32[1,256,1024]{2,1,0:T(8,128)}, u32[]{:S(2)}) copy-start(f32[1,256,1024]{2,1,0:T(8,128)} %param.8) | copy-start | bytes 3145732
  7.2 50.8 %all-gather.4.cloned.1.call-start = ((), (), s32[]{:S(2)}) async-start(), calls=%async_computation | async-start | bytes 2621440 | tf_op jit(solution)/shard_map/all_gather | solution.py:22
  7.9 99.4 %all-gather.6.cloned.1.call-start = ((), (), s32[]{:S(2)}) async-start(), calls=%async_computation.1 | async-start | bytes 2621440 | tf_op jit(solution)/shard_map/all_gather | solution.py:38
  58.0 6.6 %copy-start.1 = (bf16[1024,1024]{1,0:T(8,128)(2,1)S(1)}, bf16[1024,1024]{1,0:T(8,128)(2,1)}, u32[]{:S(2)}) copy-start(bf16[1024,1024]{1,0:T(8,128)(2,1)} %all-gather.4.cloned.1.call-done) | copy-start | bytes 6291460
  64.6 3.1 %copy-start.2 = (bf16[256,1024]{1,0:T(8,128)(2,1)S(1)}, bf16[256,1024]{1,0:T(8,128)(2,1)}, u32[]{:S(2)}) copy-start(bf16[256,1024]{1,0:T(8,128)(2,1)} %param.5) | copy-start | bytes 1572868
  64.6 3.1 %copy-start.3 = (f32[1,256,1024]{2,1,0:T(8,128)S(1)}, f32[1,256,1024]{2,1,0:T(8,128)}, u32[]{:S(2)}) copy-start(f32[1,256,1024]{2,1,0:T(8,128)} %param.6) | copy-start | bytes 3145732
Sparse Core Ops, SparseCore 0:
  9.6 48.3 all-gather.3
  62.8 44.4 all-gather.5
